TPU v7x, 32 devices: a whole 2x2x4 slice. The times are simulated.
32 devices in a mesh: ctx: 8 (over y, x, core), tensor: 4 (over z).
Axes of the slice: x: 2, y: 2, z: 4, core: 2. Of those that a mesh axis runs over, the one named last changes fastest.
Arguments:
- queries: bfloat16 [8192, 4096], P('ctx', 'tensor'), may hold values from -6 to 6
- keys: bfloat16 [8192, 4096], P('ctx', 'tensor'), may hold values from -6 to 6
- values: bfloat16 [8192, 4096], P('ctx', 'tensor'), may hold values from -6 to 6
- doc_ids: int32 [8192], P('ctx'), may hold values from 0 to 7, never falling along the last dimension, each value on 1 to 4096 neighbouring positions
- out_weight: bfloat16 [4096, 6144], P('tensor'), may hold values from -0.125 to 0.125
- grad_out: bfloat16 [8192, 6144], P('ctx', 'tensor'), may hold values from -6 to 6
Outputs:
- attended: bfloat16 [8192, 6144], P('ctx', 'tensor')
- grad_queries: bfloat16 [8192, 4096], P('ctx', 'tensor')
- grad_keys: bfloat16 [8192, 4096], P('ctx', 'tensor')
- grad_values: bfloat16 [8192, 4096], P('ctx', 'tensor')
- grad_weight: float32 [4096, 6144], P('tensor', 'ctx')
Inputs may be any that keep to these rules, and one draw needn't show every extreme that they name: `doc_ids`: never falling along the sequence; each document has 1 to 4096 positions, and one has exactly 4096.
All inputs are finite; a program needn't handle non-finite values.
Results may differ from a plain program's by a relative error of at most 0.015.
Values may be sent and summed in bfloat16 or wider, within the bound.
A program may use at most 192 MiB of HBM per device.

v0:
```python
import jax
import jax.numpy as jnp
from jax import lax
from jax.sharding import PartitionSpec as P

HEAD = 128
careful = lax.Precision.HIGH
epsilon = 1e-06


def prefix(value, axis, combine, identity, reverse):
    length, place = (lax.axis_size(axis), lax.axis_index(axis))
    everything = jax.tree.map(
        lambda part, kind: lax.all_gather(part.astype(kind), axis),
        value,
        (jnp.bfloat16, jnp.bfloat16),
    )
    start = jax.tree.map(
        lambda part, zero: jnp.broadcast_to(jnp.asarray(zero, part.dtype), part.shape),
        value,
        identity,
    )

    def turn(k, before):
        at = length - 1 - k if reverse else k
        reached = at > place if reverse else at < place
        new = combine(
            before, jax.tree.map(lambda part, own: part[at].astype(own.dtype), everything, value)
        )
        return jax.tree.map(lambda a, b: jnp.where(reached, a, b), new, before)

    return lax.fori_loop(0, length, turn, start)


def joined_state(earlier, later):
    earlier_doc, earlier_state = earlier
    later_doc, later_state = later
    vacant = later_doc < 0
    keeping = (earlier_doc == later_doc) | vacant
    doc_result = jnp.where(vacant, earlier_doc, later_doc)
    state_result = later_state + jnp.where(keeping, earlier_state, jnp.zeros_like(earlier_state))
    return (doc_result, state_result)


def carried(doc_cell, state, backward):
    identity = (jnp.full((1, 1, 1), -1.0, jnp.float32), jnp.zeros_like(state))
    if backward:
        doc_in, state_in = prefix((doc_cell, state), "ctx", joined_state, identity, True)
    else:
        doc_in, state_in = prefix((doc_cell, state), "ctx", joined_state, identity, False)
    return (doc_in.reshape(()), state_in)


def body(queries, keys, values, doc_ids, out_weight, grad_out):
    rows = queries.shape[0]
    head_size = HEAD
    heads_here = queries.shape[1] // head_size
    query_rows = queries.reshape(rows, heads_here, head_size)
    key_rows = keys.reshape(rows, heads_here, head_size)
    value_rows = values.reshape(rows, heads_here, head_size)
    doc_float = doc_ids.astype(jnp.float32)
    order = jnp.arange(rows)
    mask = ((order[:, None] >= order[None, :]) & (doc_float[:, None] == doc_float[None, :])).astype(
        jnp.float32
    )
    scores = (
        jnp.einsum("the,uhe->htu", query_rows, key_rows, preferred_element_type=jnp.float32)
        * mask[None]
    )
    local = jnp.einsum(
        "htu,uhf->thf", scores, value_rows, precision=careful, preferred_element_type=jnp.float32
    )
    tail_mask = (doc_float == doc_float[-1]).astype(jnp.bfloat16)[:, None, None]
    tail_state = jnp.einsum(
        "uhe,uhf->hef", key_rows * tail_mask, value_rows, preferred_element_type=jnp.float32
    )
    last_doc, state_in = carried(doc_float[-1].reshape(1, 1, 1), tail_state, False)
    joined = (doc_float == last_doc).astype(jnp.float32)[:, None, None]
    opened = local + joined * jnp.einsum(
        "the,hef->thf", query_rows, state_in, precision=careful, preferred_element_type=jnp.float32
    )
    inverse = lax.rsqrt(jnp.mean(opened * opened, axis=-1, keepdims=True) + epsilon)
    normed = opened * inverse
    normed_low = normed.reshape(rows, heads_here * head_size).astype(jnp.bfloat16)
    partial_out = jnp.dot(normed_low, out_weight, preferred_element_type=jnp.float32)
    attended = lax.psum_scatter(
        partial_out.astype(jnp.bfloat16), "tensor", scatter_dimension=1, tiled=True
    )
    grad_whole = lax.all_gather(grad_out, "tensor", axis=1, tiled=True)
    grad_normed = lax.dot_general(
        grad_whole, out_weight, (((1,), (1,)), ((), ())), preferred_element_type=jnp.float32
    )
    weight_term = lax.dot_general(
        normed_low, grad_whole, (((0,), (0,)), ((), ())), preferred_element_type=jnp.float32
    )
    grad_weight = lax.psum_scatter(
        weight_term.astype(jnp.bfloat16), "ctx", scatter_dimension=1, tiled=True
    ).astype(jnp.float32)
    grad_normed = grad_normed.reshape(rows, heads_here, head_size)
    grad_opened = inverse * (
        grad_normed - normed * jnp.mean(grad_normed * normed, axis=-1, keepdims=True)
    )
    head_mask = (doc_float == doc_float[0]).astype(jnp.bfloat16)[:, None, None]
    head_state = jnp.einsum(
        "the,thf->hef",
        query_rows * head_mask,
        grad_opened,
        precision=careful,
        preferred_element_type=jnp.float32,
    )
    first_doc, state_back = carried(doc_float[0].reshape(1, 1, 1), head_state, True)
    starts = (doc_float == first_doc).astype(jnp.float32)[:, None, None]
    grad_scores = (
        jnp.einsum(
            "thf,uhf->htu",
            grad_opened,
            value_rows,
            precision=careful,
            preferred_element_type=jnp.float32,
        )
        * mask[None]
    )
    grad_query = jnp.einsum(
        "htu,uhe->the", grad_scores, key_rows, precision=careful, preferred_element_type=jnp.float32
    ) + joined * jnp.einsum(
        "thf,hef->the", grad_opened, state_in, precision=careful, preferred_element_type=jnp.float32
    )
    grad_key = jnp.einsum(
        "htu,the->uhe",
        grad_scores,
        query_rows,
        precision=careful,
        preferred_element_type=jnp.float32,
    ) + starts * jnp.einsum(
        "uhf,hef->uhe",
        value_rows,
        state_back,
        precision=careful,
        preferred_element_type=jnp.float32,
    )
    grad_value = jnp.einsum(
        "htu,thf->uhf", scores, grad_opened, precision=careful, preferred_element_type=jnp.float32
    ) + starts * jnp.einsum(
        "uhe,hef->uhf", key_rows, state_back, precision=careful, preferred_element_type=jnp.float32
    )
    flat = heads_here * head_size
    return (
        attended,
        grad_query.reshape(rows, flat).astype(jnp.bfloat16),
        grad_key.reshape(rows, flat).astype(jnp.bfloat16),
        grad_value.reshape(rows, flat).astype(jnp.bfloat16),
        grad_weight,
    )


def solution(mesh):
    return jax.shard_map(
        body,
        mesh=mesh,
        in_specs=(
            P("ctx", "tensor"),
            P("ctx", "tensor"),
            P("ctx", "tensor"),
            P("ctx"),
            P("tensor", None),
            P("ctx", "tensor"),
        ),
        out_specs=(
            P("ctx", "tensor"),
            P("ctx", "tensor"),
            P("ctx", "tensor"),
            P("ctx", "tensor"),
            P("tensor", "ctx"),
        ),
        check_vma=False,
    )
```

profile of v0, /device:TPU:0, one launch (start us, length us, event | category | flops | bytes accessed | tf_op | source)
XLA Modules:
  0.0 642.6 jit_solution(15173689273183936138)
XLA Ops:
  7.2 0.8 convert_element_type.118
  8.6 3.6 copy.65
  12.2 4.1 copy.36
  16.3 1.3 compare_convert_fusion.1
  17.6 3.1 fusion.46
  20.8 0.7 all-gather.8.cloned.1.call-update
  22.7 1.4 dynamic-update-slice
  24.1 1.4 dynamic-update-slice.1
  25.5 15.8 %all-reduce.2 = (bf16[8]{0:T(256)(128)(2,1)S(1)}, bf16[8]{0:T(256)(128)(2,1)}) all-reduce(bf16[8]{0:T(256)(128)(2,1)S(1)} %dynamic-update-slice, bf16[8]{0:T(256)(128)(2,1)S(1)} %dynamic-update-slice.1), channel_id=2, replica_groups=mesh['ctx'=8,'tensor'=4] {'ctx'}, use_global_device_ids=true, to_apply=%add | all-reduce | flops 16 | bytes 64
  41.3 4.0 copy.62
  45.3 2.8 fusion.17
  48.1 1.0 copy-done.7
  49.1 14.8 %fusion.32 = f32[8,1024,1024]{2,1,0:T(8,128)} fusion(bf16[1024,8,128]{0,2,1:T(8,128)(2,1)S(1)} %bitcast.128, bf16[1024,1024]{1,0:T(8,128)(2,1)S(1)} %copy-done.7), kind=kOutput, calls=%fused_computation.41 | convolution fusion | flops 2147483648 | bytes 37748736 | tf_op jit(solution)/shard_map/the,uhe->htu/dot_general | solution.py:67
  63.9 31.0 %while.34 = (s32[]{:T(128)}, f32[1,1,1]{2,1,0:T(1,128)}, f32[8,128,128]{2,1,0:T(8,128)S(1)}, s32[]{:T(128)}, bf16[8,1,1,1]{0,3,2,1:T(2,128)(2,1)S(1)}, /*index=5...) while((s32[]{:T(128)}, f32[1,1,1]{2,1,0:T(1,128)}, ...), condition=%wide.region_1.2_spmd.clone, body=%wide.region_0.1_spmd.clone.sunk | while | flops 655369 | bytes 1310887 | solution.py:32
  63.9 0.6 constant_dynamic-slice_fusion.4
  65.8 1.3 fusion.83
  67.8 0.7 constant_dynamic-slice_fusion.4
  69.7 1.3 fusion.83
  71.7 0.7 constant_dynamic-slice_fusion.4
  73.6 1.3 fusion.83
  75.5 0.7 constant_dynamic-slice_fusion.4
  77.5 1.3 fusion.83
  79.4 0.7 constant_dynamic-slice_fusion.4
  81.4 1.3 fusion.83
  83.3 0.7 constant_dynamic-slice_fusion.4
  85.2 1.3 fusion.83
  87.2 0.7 constant_dynamic-slice_fusion.4
  89.1 1.3 fusion.83
  91.1 0.7 constant_dynamic-slice_fusion.4
  93.0 1.3 fusion.83
  94.9 4.9 fusion.55
  99.8 21.0 %multiply_reduce_fusion.1 = (f32[1024,8]{0,1:T(8,128)S(1)}, f32[1024,8,128]{0,2,1:T(8,128)}) fusion(f32[8,128,1024]{2,1,0:T(8,128)} %fusion.55, f32[1024]{0:T(1024)S(1)} %compare_convert_fusion.2, f32[8,1024,1024]{2,1,0:T(8,128)} %fusion.32, f32[1024,1024]{1,0:T(8,128)} %fusion.17, bf16[1024,1024]{1,0:T(8,128)(2,1)S(1)} %copy-done), kind=kOutput, calls=%fused_computation.28 | convolution fusion | flops 6455025664 | bytes 48271360 | tf_op jit(solution)/shard_map/htu,uhf->thf/dot_general | solution.py:70
  120.8 150.5 %all-gather.8.cloned.1.call-done = bf16[1024,6144]{1,0:T(8,128)(2,1)} async-done(((bf16[1024,1536]{1,0:T(8,128)(2,1)}), bf16[1024,6144]{1,0:T(8,128)(2,1)}) %all-gather.8.cloned.1.call-update) | async-done | bytes 12582928 | tf_op jit(solution)/shard_map/all_gather | solution.py:89
  271.3 21.3 %multiply_reduce_fusion = (f32[1024,8]{0,1:T(8,128)S(1)}, f32[1024,1024]{0,1:T(8,128)S(1)}) fusion(f32[1024,8,128]{0,2,1:T(8,128)} %get-tuple-element.385, f32[1024,8]{0,1:T(8,128)S(1)} %add_rsqrt_fusion, bf16[1024,6144]{1,0:T(8,128)(2,1)} %all-gather.8.cloned.1.call-done, bf16[1024,6144]{1,0:T(8,128)(2,1)} %param.14), kind=kOutput, calls=%fused_computation.27 | convolution fusion | flops 12888039424 | bytes 33619968 | tf_op jit(solution)/shard_map/dot_general | solution.py:90
  292.7 3.0 subtract_multiply_fusion
  295.6 2.0 copy-done.3
  297.6 2.1 fusion.43
  299.7 20.9 %convolution_convert_fusion = bf16[1024,6144]{1,0:T(8,128)(2,1)} fusion(bf16[1024,1024]{0,1:T(8,128)(2,1)} %bitcast.136, bf16[1024,6144]{1,0:T(8,128)(2,1)} %all-gather.8.cloned.1.call-done), kind=kOutput, calls=%fused_computation.18 | convolution fusion | flops 12891193344 | bytes 27262976 | tf_op jit(solution)/shard_map/dot_general | solution.py:93
  320.7 22.6 %convolution_convert_fusion.1 = bf16[1024,6144]{1,0:T(8,128)(2,1)} fusion(bf16[1024,1024]{0,1:T(8,128)(2,1)} %bitcast.137, bf16[1024,6144]{1,0:T(8,128)(2,1)} %param.14), kind=kOutput, calls=%fused_computation.19 | convolution fusion | flops 12891193344 | bytes 27262976 | tf_op jit(solution)/shard_map/dot_general | solution.py:85
  343.4 7.2 %fusion.56 = f32[8,128,1024]{2,1,0:T(8,128)} fusion(f32[8,128,128]{2,1,0:T(8,128)S(1)} %get-tuple-element.271, f32[1024,8,128]{0,2,1:T(8,128)} %copy-done.3), kind=kOutput, calls=%fused_computation.67 | convolution fusion | flops 805306368 | bytes 8912896 | tf_op jit(solution)/shard_map/thf,hef->the/dot_general | solution.py:125
  350.6 18.5 %fusion.27 = f32[8,1024,1024]{2,1,0:T(8,128)} fusion(f32[1024,8,128]{0,2,1:T(8,128)} %copy-done.3, bf16[1024,1024]{1,0:T(8,128)(2,1)S(1)} %copy-done), kind=kOutput, calls=%fused_computation.36 | convolution fusion | flops 6442450944 | bytes 39845888 | tf_op jit(solution)/shard_map/thf,uhf->htu/dot_general | solution.py:114
  369.2 19.0 %fusion.15 = bf16[1024,8,128]{0,2,1:T(8,128)(2,1)} fusion(f32[8,128,1024]{2,1,0:T(8,128)} %fusion.56, bf16[1024,8,128]{0,2,1:T(8,128)(2,1)} %copy.36, f32[8,1024,1024]{2,1,0:T(8,128)} %fusion.27, f32[1024,1024]{1,0:T(8,128)S(1)} %copy-done.1, f32[1024]{0:T(1024)S(1)} %compare_convert_fusion.2), kind=kOutput, calls=%fused_computation.23 | convolution fusion | flops 6453985280 | bytes 46141440 | tf_op jit(solution)/shard_map/htu,uhe->the/dot_general | solution.py:123
  388.1 3.9 copy.52
  392.1 19.4 %fusion.6 = f32[8,128,1024]{2,1,0:T(8,128)} fusion(f32[1024,8,128]{0,2,1:T(8,128)} %copy-done.3, f32[8,1024,1024]{2,1,0:T(8,128)} %fusion.32, f32[1024,1024]{1,0:T(8,128)} %fusion.17), kind=kOutput, calls=%fused_computation.10 | convolution fusion | flops 6450839552 | bytes 46137344 | tf_op jit(solution)/shard_map/htu,thf->uhf/dot_general | solution.py:141
  411.4 31.1 %while.35 = (s32[]{:T(128)}, f32[1,1,1]{2,1,0:T(1,128)}, f32[8,128,128]{2,1,0:T(8,128)S(1)}, s32[]{:T(128)}, bf16[8,1,1,1]{0,3,2,1:T(2,128)(2,1)S(1)}, /*index=5...) while((s32[]{:T(128)}, f32[1,1,1]{2,1,0:T(1,128)}, ...), condition=%wide.region_6.7_spmd.clone, body=%wide.region_5.6_spmd.clone.sunk | while | flops 655373 | bytes 1310949 | solution.py:32
  411.5 0.6 constant_dynamic-slice_fusion.5
  413.4 1.3 fusion.84
  415.3 0.6 constant_dynamic-slice_fusion.5
  417.2 1.3 fusion.84
  421.1 1.3 fusion.84
  424.9 1.3 fusion.84
  428.8 1.3 fusion.84
  432.7 1.3 fusion.84
  436.6 1.3 fusion.84
  440.4 1.3 fusion.84
  442.5 5.7 add_convert_fusion
  448.2 3.9 copy.54
  452.2 1.3 fusion.25
  453.5 0.9 copy-done.2
  454.3 0.7 copy-done.6
  455.0 17.1 %fusion.14 = bf16[1024,8,128]{0,2,1:T(8,128)(2,1)} fusion(f32[8,128,1024]{2,1,0:T(8,128)S(1)} %fusion.25, bf16[1024,8,128]{0,2,1:T(8,128)(2,1)S(1)} %bitcast.130, f32[8,1024,1024]{2,1,0:T(8,128)} %fusion.27, f32[1024,1024]{1,0:T(8,128)S(1)} %copy-done.2, f32[1024]{0:T(1024)S(1)} %compare_convert_fusion), kind=kOutput, calls=%fused_computation.21 | convolution fusion | flops 6453985280 | bytes 46141440 | tf_op jit(solution)/shard_map/htu,the->uhe/dot_general | solution.py:128
  472.1 4.0 copy.53
  476.1 3.3 convert_element_type.139
  479.4 156.5 %reduce-scatter.3.cloned.1.call-done = bf16[1024,1536]{1,0:T(8,128)(2,1)} async-done(((bf16[1024,6144]{1,0:T(8,128)(2,1)}), bf16[1024,1536]{1,0:T(8,128)(2,1)}) %reduce-scatter.3.cloned.1.call-update) | async-done | bytes 3145744 | tf_op jit(solution)/shard_map/reduce_scatter | solution.py:86
  (53 shorter events, 5.6 us)
Async XLA Ops:
  7.2 10.4 %copy-start = (bf16[1024,1024]{1,0:T(8,128)(2,1)S(1)}, bf16[1024,1024]{1,0:T(8,128)(2,1)}, u32[]{:S(2)}) copy-start(bf16[1024,1024]{1,0:T(8,128)(2,1)} %param.12) | copy-start | bytes 6291460
  7.2 56.7 %all-gather.10.cloned.1.call-start = ((), (), s32[]{:S(2)}) async-start(), calls=%async_computation.5 | async-start | bytes 2359296 | tf_op jit(solution)/shard_map/all_gather | solution.py:14
  8.6 7.7 %copy-start.10 = (s32[1024]{0:T(1024)S(1)}, s32[1024]{0:T(1024)}, u32[]{:S(2)}) copy-start(s32[1024]{0:T(1024)} %param.13) | copy-start | bytes 12292
  17.6 3.9 copy-start.13
  20.7 250.5 %all-gather.8.cloned.1.call-start = ((), (), s32[]{:S(2)}) async-start(), calls=%async_computation.3 | async-start | bytes 15728640 | tf_op jit(solution)/shard_map/all_gather | solution.py:89
  21.5 389.9 %all-gather.12.cloned.1.call-start = ((), (), s32[]{:S(2)}) async-start(), calls=%async_computation.6 | async-start | bytes 2359296 | tf_op jit(solution)/shard_map/all_gather | solution.py:14
  45.3 2.8 copy-start.4
  45.3 3.8 copy-start.7
  271.3 21.3 %copy-start.8 = (f32[1024,8,128]{0,2,1:T(8,128)S(1)}, f32[1024,8,128]{0,2,1:T(8,128)}, u32[]{:S(2)}) copy-start(f32[1024,8,128]{0,2,1:T(8,128)} %get-tuple-element.385) | copy-start | bytes 12582916
  292.6 5.0 copy-start.5
  295.6 2.0 copy-start.3
  299.7 176.4 %reduce-scatter.5.cloned.1.call-start = ((), (), s32[]{:S(2)}) async-start(), calls=%async_computation.4 | async-start | bytes 14155776 | tf_op jit(solution)/shard_map/reduce_scatter | solution.py:96
  320.7 315.2 %reduce-scatter.3.cloned.1.call-start = ((), (), s32[]{:S(2)}) async-start(), calls=%async_computation.2 | async-start | bytes 15728640 | tf_op jit(solution)/shard_map/reduce_scatter | solution.py:86
  350.6 18.5 %copy-start.1 = (f32[1024,1024]{1,0:T(8,128)S(1)}, f32[1024,1024]{1,0:T(8,128)}, u32[]{:S(2)}) copy-start(f32[1024,1024]{1,0:T(8,128)} %fusion.17) | copy-start | bytes 12582916
  392.1 19.4 %copy-start.9 = (f32[8,128,128]{2,1,0:T(8,128)S(1)}, f32[8,128,128]{2,1,0:T(8,128)}, u32[]{:S(2)}) copy-start(f32[8,128,128]{2,1,0:T(8,128)} %custom-call.1) | copy-start | bytes 1572868
  392.1 19.4 %copy-start.12 = (bf16[8]{0:T(256)(128)(2,1)S(1)}, bf16[8]{0:T(256)(128)(2,1)}, u32[]{:S(2)}) copy-start(bf16[8]{0:T(256)(128)(2,1)} %get-tuple-element.375) | copy-start | bytes 52
  411.4 31.1 %copy-start.11 = (s32[1024]{0:T(1024)S(1)}, s32[1024]{0:T(1024)}, u32[]{:S(2)}) copy-start(s32[1024]{0:T(1024)} %param.13) | copy-start | bytes 12292
  452.2 2.2 copy-start.2
  452.2 2.9 copy-start.6
Sparse Core Ops, SparseCore 0:
  20.9 30.5 all-gather.9
  53.1 218.1 all-gather.7
  299.8 25.9 all-gather.11
  329.2 91.9 reduce-scatter.4
  423.9 211.8 reduce-scatter.2
where the time goes:
time: 652 us; the launch traced here: 643 us
  waiting for transfers between devices  308 us (47%)
  matrix products  199 us (31%)
  local copies, waits for them, and re-layouts  42.5 us (7%)
  loops' own time  31.9 us (5%)
  other arithmetic  31.5 us (5%)
  blocking collectives  15.8 us (2%)
  between operations  14.1 us (2%)
    reduce_scatter x1, waiting for transfers between devices, body(): lax.psum_scatter(partial_out.astype(jnp.bfloat16), 'tensor', scatter_dime...  156 us
    all_gather x1, waiting for transfers between devices, body(): grad_whole = lax.all_gather(grad_out, 'tensor', axis=1, tiled=True)  150 us
    another operation x2, loops' own time, prefix(): return lax.fori_loop(0, length, turn, start)  31.9 us
    unnamed x37, local copies, waits for them, and re-layouts  23.4 us
    dot_general x1, matrix products, body(): jnp.dot(normed_low, out_weight, preferred_element_type=jnp.float32)  22.6 us
    dot_general x1, matrix products, body(): lax.dot_general(grad_whole, out_weight, (((1,), (1,)), ((), ())), preferr...  21.3 us
    dot_general x1, matrix products, body(): jnp.einsum('htu,uhf->thf', scores, value_rows, precision=careful, preferr...  21 us
    dot_general x1, matrix products, body(): lax.dot_general(normed_low, grad_whole, (((0,), (0,)), ((), ())), preferr...  20.9 us
  transfers between devices with their start and end apart: 5, of which 2 were waited for; matrix products, arithmetic and copies ran while one was open for 36% of the time, Pallas kernels for 0%

commit v1 on v0

--- a/solution.py
+++ b/solution.py
@@ -86,7 +86,18 @@
     attended = lax.psum_scatter(
         partial_out.astype(jnp.bfloat16), "tensor", scatter_dimension=1, tiled=True
     )
-    grad_whole = lax.all_gather(grad_out, "tensor", axis=1, tiled=True)
+    n_slots = lax.psum(1, axis_name="tensor")
+    f_next = grad_out
+    xs_all = [f_next]
+    jj = 1
+    odd = sorted(((t, (t + 1) % n_slots) for t in range(n_slots)))
+    while jj < n_slots:
+        f_next = lax.ppermute(f_next, axis_name="tensor", perm=odd)
+        xs_all.insert(0, f_next)
+        jj += 1
+    grad_whole = jnp.roll(
+        jnp.concatenate(xs_all, axis=1), (lax.axis_index("tensor") + 1) * grad_out.shape[1], axis=1
+    )
     grad_normed = lax.dot_general(
         grad_whole, out_weight, (((1,), (1,)), ((), ())), preferred_element_type=jnp.float32
     )

time: 652 us -> 627 us (0.962)
  waiting for transfers between devices: 308 us -> 258 us
  local copies, waits for them, and re-layouts: 42.5 us -> 69.2 us
    all_gather x1 -> x0, waiting for transfers between devices: 150 us -> none  [body(): grad_whole = lax.all_gather(grad_out, 'tensor', axis=1, tiled=True)]
    ppermute x0 -> x3, waiting for transfers between devices: none -> 102 us  [body(): f_next = lax.ppermute(f_next, axis_name='tensor', perm=odd)]
    unnamed x37 -> x42, local copies, waits for them, and re-layouts: 23.4 us -> 48.6 us
  transfers between devices with their start and end apart: 5 -> 7, of which waited for: 2 -> 4; matrix products, arithmetic and copies ran while one was open for 36% -> 39% of each run, Pallas kernels for 0% -> 0%
where the time goes in v1:
time: 627 us; the launch traced here: 619 us
  waiting for transfers between devices  258 us (41%)
  matrix products  199 us (32%)
  local copies, waits for them, and re-layouts  69.2 us (11%)
  other arithmetic  30.8 us (5%)
  loops' own time  30 us (5%)
  blocking collectives  14.3 us (2%)
  between operations  14.2 us (2%)
    reduce_scatter x1, waiting for transfers between devices, body(): lax.psum_scatter(partial_out.astype(jnp.bfloat16), 'tensor', scatter_dime...  156 us
    ppermute x3, waiting for transfers between devices, body(): f_next = lax.ppermute(f_next, axis_name='tensor', perm=odd)  102 us
    unnamed x42, local copies, waits for them, and re-layouts  48.6 us
    another operation x2, loops' own time, prefix(): return lax.fori_loop(0, length, turn, start)  30 us
    dot_general x1, matrix products, body(): jnp.dot(normed_low, out_weight, preferred_element_type=jnp.float32)  22.8 us
    dot_general x1, matrix products, body(): lax.dot_general(normed_low, grad_whole, (((0,), (0,)), ((), ())), preferr...  21.3 us
    dot_general x1, matrix products, body(): jnp.einsum('htu,uhf->thf', scores, value_rows, precision=careful, preferr...  20.9 us
    select_n x16, other arithmetic, turn(): return jax.tree.map(lambda a, b: jnp.where(reached, a, b), new, before)  20.4 us
  transfers between devices with their start and end apart: 7, of which 4 were waited for; matrix products, arithmetic and copies ran while one was open for 39% of the time, Pallas kernels for 0%

profile of v1, /device:TPU:0, one launch (start us, length us, event | category | flops | bytes accessed | tf_op | source)
XLA Modules:
  0.0 618.7 jit_solution(11062554896783065377)
XLA Ops:
  7.2 3.1 collective-permute-start
  10.3 0.7 convert_element_type.118
  11.0 3.6 copy.65
  14.6 4.1 copy.36
  19.3 1.3 compare_convert_fusion.1
  20.6 3.1 fusion.49
  23.8 3.9 copy.62
  28.9 1.4 dynamic-update-slice.1
  30.4 1.4 dynamic-update-slice
  31.8 49.0 %collective-permute-done = bf16[1024,1536]{1,0:T(8,128)(2,1)} collective-permute-done((bf16[1024,1536]{1,0:T(8,128)(2,1)}, bf16[1024,1536]{1,0:T(8,128)(2,1)}, u32[]{:S(2)}, u32[]{:S(2)}) %collective-permute-start) | collective-permute-done | bytes 3145760 | tf_op jit(solution)/shard_map/ppermute | solution.py:95
  80.8 17.8 %fusion.35 = f32[8,1024,1024]{2,1,0:T(8,128)} fusion(bf16[1024,8,128]{0,2,1:T(8,128)(2,1)} %bitcast.125, bf16[1024,1024]{1,0:T(8,128)(2,1)} %param.11), kind=kOutput, calls=%fused_computation.44 | convolution fusion | flops 2147483648 | bytes 37748736 | tf_op jit(solution)/shard_map/the,uhe->htu/dot_general | solution.py:67
  98.6 14.3 %all-reduce.2 = (bf16[8]{0:T(256)(128)(2,1)S(1)}, bf16[8]{0:T(256)(128)(2,1)}) all-reduce(bf16[8]{0:T(256)(128)(2,1)S(1)} %dynamic-update-slice, bf16[8]{0:T(256)(128)(2,1)S(1)} %dynamic-update-slice.1), channel_id=2, replica_groups=mesh['ctx'=8,'tensor'=4] {'ctx'}, use_global_device_ids=true, to_apply=%add | all-reduce | flops 16 | bytes 64
  112.9 2.6 fusion.20
  115.5 28.7 %while.34 = (s32[]{:T(128)}, f32[1,1,1]{2,1,0:T(1,128)}, f32[8,128,128]{2,1,0:T(8,128)S(1)}, s32[]{:T(128)}, bf16[8,1,1,1]{0,3,2,1:T(2,128)(2,1)S(1)}, /*index=5...) while((s32[]{:T(128)}, f32[1,1,1]{2,1,0:T(1,128)}, ...), condition=%wide.region_1.2_spmd.clone, body=%wide.region_0.1_spmd.clone.sunk | while | flops 655369 | bytes 1310895 | solution.py:32
  117.8 1.3 fusion.86
  121.3 1.3 fusion.86
  124.9 1.3 fusion.86
  128.5 1.3 fusion.86
  132.1 1.3 fusion.86
  135.7 1.3 fusion.86
  139.3 1.3 fusion.86
  142.9 1.3 fusion.86
  144.2 8.0 %collective-permute-done.1 = bf16[1024,1536]{1,0:T(8,128)(2,1)} collective-permute-done((bf16[1024,1536]{1,0:T(8,128)(2,1)}, bf16[1024,1536]{1,0:T(8,128)(2,1)}, u32[]{:S(2)}, u32[]{:S(2)}) %collective-permute-start.1) | collective-permute-done | bytes 3145760 | tf_op jit(solution)/shard_map/ppermute | solution.py:95
  152.3 4.8 fusion.60
  157.2 20.9 %multiply_reduce_fusion.1 = (f32[1024,8]{0,1:T(8,128)S(1)}, f32[1024,8,128]{0,2,1:T(8,128)}) fusion(f32[8,128,1024]{2,1,0:T(8,128)} %fusion.60, f32[1024]{0:T(1024)S(1)} %compare_convert_fusion.2, f32[8,1024,1024]{2,1,0:T(8,128)} %fusion.35, f32[1024,1024]{1,0:T(8,128)} %fusion.20, bf16[1024,1024]{1,0:T(8,128)(2,1)S(1)} %copy-done), kind=kOutput, calls=%fused_computation.31 | convolution fusion | flops 6455025664 | bytes 48271360 | tf_op jit(solution)/shard_map/htu,uhf->thf/dot_general | solution.py:70
  178.1 44.8 %collective-permute-done.2 = bf16[1024,1536]{1,0:T(8,128)(2,1)} collective-permute-done((bf16[1024,1536]{1,0:T(8,128)(2,1)}, bf16[1024,1536]{1,0:T(8,128)(2,1)}, u32[]{:S(2)}, u32[]{:S(2)}) %collective-permute-start.2) | collective-permute-done | bytes 3145760 | tf_op jit(solution)/shard_map/ppermute | solution.py:95
  222.8 3.8 constant_dynamic-update-slice_fusion.7
  226.6 3.8 constant_dynamic-update-slice_fusion.6
  230.4 3.9 constant_dynamic-update-slice_fusion.5
  234.3 1.9 constant_dynamic-update-slice_fusion.4
  236.3 3.8 constant_dynamic-update-slice_fusion.3
  240.0 3.8 constant_dynamic-update-slice_fusion.2
  243.8 3.7 constant_dynamic-update-slice_fusion.1
  247.6 1.9 constant_dynamic-update-slice_fusion
  249.5 1.4 copy-done.6
  250.9 18.5 %multiply_reduce_fusion = (f32[1024,8]{0,1:T(8,128)S(1)}, f32[1024,1024]{0,1:T(8,128)S(1)}) fusion(f32[1024,8,128]{0,2,1:T(8,128)S(1)} %copy-done.6, f32[1024,8]{0,1:T(8,128)S(1)} %add_rsqrt_fusion, bf16[1024,6144]{1,0:T(8,128)(2,1)} %param.14, bf16[1024,12288]{1,0:T(8,128)(2,1)} %constant_dynamic-update-slice_fusion, s32[]{:T(128)S(6)} %select_n.132), kind=kOutput, calls=%fused_computation.30 | convolution fusion | flops 12888039424 | bytes 33619972 | tf_op jit(solution)/shard_map/dot_general | solution.py:101
  269.4 2.6 subtract_multiply_fusion
  272.0 2.0 copy-done.3
  273.9 2.1 fusion.46
  276.1 21.3 %convolution_convert_fusion = bf16[1024,6144]{1,0:T(8,128)(2,1)} fusion(bf16[1024,1024]{0,1:T(8,128)(2,1)} %bitcast.134, bf16[1024,12288]{1,0:T(8,128)(2,1)} %constant_dynamic-update-slice_fusion, s32[]{:T(128)S(6)} %select_n.132), kind=kOutput, calls=%fused_computation.18 | convolution fusion | flops 12891193344 | bytes 27262980 | tf_op jit(solution)/shard_map/dot_general | solution.py:104
  297.5 22.8 %convolution_convert_fusion.1 = bf16[1024,6144]{1,0:T(8,128)(2,1)} fusion(bf16[1024,1024]{0,1:T(8,128)(2,1)} %bitcast.135, bf16[1024,6144]{1,0:T(8,128)(2,1)} %param.14), kind=kOutput, calls=%fused_computation.19 | convolution fusion | flops 12891193344 | bytes 27262976 | tf_op jit(solution)/shard_map/dot_general | solution.py:85
  320.3 7.2 %fusion.61 = f32[8,128,1024]{2,1,0:T(8,128)} fusion(f32[8,128,128]{2,1,0:T(8,128)S(1)} %get-tuple-element.271, f32[1024,8,128]{0,2,1:T(8,128)} %copy-done.3), kind=kOutput, calls=%fused_computation.80 | convolution fusion | flops 805306368 | bytes 8912896 | tf_op jit(solution)/shard_map/thf,hef->the/dot_general | solution.py:136
  327.5 18.3 %fusion.30 = f32[8,1024,1024]{2,1,0:T(8,128)} fusion(f32[1024,8,128]{0,2,1:T(8,128)} %copy-done.3, bf16[1024,1024]{1,0:T(8,128)(2,1)S(1)} %copy-done), kind=kOutput, calls=%fused_computation.39 | convolution fusion | flops 6442450944 | bytes 39845888 | tf_op jit(solution)/shard_map/thf,uhf->htu/dot_general | solution.py:125
  345.8 18.8 %fusion.18 = bf16[1024,8,128]{0,2,1:T(8,128)(2,1)} fusion(f32[8,128,1024]{2,1,0:T(8,128)} %fusion.61, bf16[1024,8,128]{0,2,1:T(8,128)(2,1)} %copy.36, f32[8,1024,1024]{2,1,0:T(8,128)} %fusion.30, f32[1024,1024]{1,0:T(8,128)S(1)} %copy-done.1, f32[1024]{0:T(1024)S(1)} %compare_convert_fusion.2), kind=kOutput, calls=%fused_computation.26 | convolution fusion | flops 6453985280 | bytes 46141440 | tf_op jit(solution)/shard_map/htu,uhe->the/dot_general | solution.py:134
  364.6 3.9 copy.52
  368.5 19.0 %fusion.6 = f32[8,128,1024]{2,1,0:T(8,128)} fusion(f32[1024,8,128]{0,2,1:T(8,128)} %copy-done.3, f32[8,1024,1024]{2,1,0:T(8,128)} %fusion.35, f32[1024,1024]{1,0:T(8,128)} %fusion.20), kind=kOutput, calls=%fused_computation.10 | convolution fusion | flops 6450839552 | bytes 46137344 | tf_op jit(solution)/shard_map/htu,thf->uhf/dot_general | solution.py:152
  387.6 31.1 %while.35 = (s32[]{:T(128)}, f32[1,1,1]{2,1,0:T(1,128)}, f32[8,128,128]{2,1,0:T(8,128)S(1)}, s32[]{:T(128)}, bf16[8,1,1,1]{0,3,2,1:T(2,128)(2,1)S(1)}, /*index=5...) while((s32[]{:T(128)}, f32[1,1,1]{2,1,0:T(1,128)}, ...), condition=%wide.region_6.7_spmd.clone, body=%wide.region_5.6_spmd.clone.sunk | while | flops 655373 | bytes 1310957 | solution.py:32
  390.2 1.3 fusion.87
  394.0 1.3 fusion.87
  397.9 1.3 fusion.87
  401.7 1.3 fusion.87
  405.6 1.3 fusion.87
  409.5 1.3 fusion.87
  413.3 1.3 fusion.87
  417.2 1.3 fusion.87
  418.7 5.7 add_convert_fusion
  424.4 3.9 copy.54
  428.3 1.3 fusion.28
  429.6 0.9 copy-done.2
  430.5 0.7 copy-done.5
  431.2 17.1 %fusion.17 = bf16[1024,8,128]{0,2,1:T(8,128)(2,1)} fusion(f32[8,128,1024]{2,1,0:T(8,128)S(1)} %fusion.28, bf16[1024,8,128]{0,2,1:T(8,128)(2,1)S(1)} %bitcast.128, f32[8,1024,1024]{2,1,0:T(8,128)} %fusion.30, f32[1024,1024]{1,0:T(8,128)S(1)} %copy-done.2, f32[1024]{0:T(1024)S(1)} %compare_convert_fusion), kind=kOutput, calls=%fused_computation.24 | convolution fusion | flops 6453985280 | bytes 46141440 | tf_op jit(solution)/shard_map/htu,the->uhe/dot_general | solution.py:139
  448.3 4.0 copy.53
  452.2 3.3 convert_element_type.139
  455.5 156.4 %reduce-scatter.3.cloned.1.call-done = bf16[1024,1536]{1,0:T(8,128)(2,1)} async-done(((bf16[1024,6144]{1,0:T(8,128)(2,1)}), bf16[1024,1536]{1,0:T(8,128)(2,1)}) %reduce-scatter.3.cloned.1.call-update) | async-done | bytes 3145744 | tf_op jit(solution)/shard_map/reduce_scatter | solution.py:86
  (62 shorter events, 11.7 us)
Async XLA Ops:
  7.2 13.4 %copy-start = (bf16[1024,1024]{1,0:T(8,128)(2,1)S(1)}, bf16[1024,1024]{1,0:T(8,128)(2,1)}, u32[]{:S(2)}) copy-start(bf16[1024,1024]{1,0:T(8,128)(2,1)} %param.12) | copy-start | bytes 6291460
  7.2 108.3 %all-gather.7.cloned.1.call-start = ((), (), s32[]{:S(2)}) async-start(), calls=%async_computation.4 | async-start | bytes 2359296 | tf_op jit(solution)/shard_map/all_gather | solution.py:14
  7.2 73.5 %collective-permute-start = (bf16[1024,1536]{1,0:T(8,128)(2,1)}, bf16[1024,1536]{1,0:T(8,128)(2,1)}, u32[]{:S(2)}, u32[]{:S(2)}) collective-permute-start(bf16[1024,1536]{1,0:T(8,128)(2,1)} %param.15), channel_id=1, source_target_pairs={{0,1},{1,2},{2,3},{3,0},{4,5},{5,6},{6,7},{7,4},{8,9},{9,10},{10,1... | collective-permute-start | bytes 9437192 | tf_op jit(solution)/shard_map/ppermute | solution.py:95
  11.0 8.2 %copy-start.9 = (s32[1024]{0:T(1024)S(1)}, s32[1024]{0:T(1024)}, u32[]{:S(2)}) copy-start(s32[1024]{0:T(1024)} %param.13) | copy-start | bytes 12292
  20.6 7.1 %copy-start.12 = (u32[32]{0:T(128)S(1)}, u32[32]{0:T(128)}, u32[]{:S(2)}) copy-start(u32[32]{0:T(128)} %constant.140) | copy-start | bytes 388
  23.7 363.9 %all-gather.9.cloned.1.call-start = ((), (), s32[]{:S(2)}) async-start(), calls=%async_computation.5 | async-start | bytes 2359296 | tf_op jit(solution)/shard_map/all_gather | solution.py:14
  80.8 71.4 %collective-permute-start.1 = (bf16[1024,1536]{1,0:T(8,128)(2,1)}, bf16[1024,1536]{1,0:T(8,128)(2,1)}, u32[]{:S(2)}, u32[]{:S(2)}) collective-permute-start(bf16[1024,1536]{1,0:T(8,128)(2,1)} %collective-permute-done), channel_id=1, source_target_pairs={{0,1},{1,2},{2,3},{3,0},{4,5},{5,6},{6,7},{7,4},{8,9},{9,10},{10,1... | collective-permute-start | bytes 9437192 | tf_op jit(solution)/shard_map/ppermute | solution.py:95
  152.2 70.7 %collective-permute-start.2 = (bf16[1024,1536]{1,0:T(8,128)(2,1)}, bf16[1024,1536]{1,0:T(8,128)(2,1)}, u32[]{:S(2)}, u32[]{:S(2)}) collective-permute-start(bf16[1024,1536]{1,0:T(8,128)(2,1)} %collective-permute-done.1), channel_id=1, source_target_pairs={{0,1},{1,2},{2,3},{3,0},{4,5},{5,6},{6,7},{7,4},{8,9},{9,10},{10,1... | collective-permute-start | bytes 9437192 | tf_op jit(solution)/shard_map/ppermute | solution.py:95
  230.4 3.9 copy-start.8
  247.6 3.3 copy-start.6
  269.4 4.5 copy-start.4
  272.0 2.0 copy-start.3
  276.0 176.2 %reduce-scatter.5.cloned.1.call-start = ((), (), s32[]{:S(2)}) async-start(), calls=%async_computation.3 | async-start | bytes 14155776 | tf_op jit(solution)/shard_map/reduce_scatter | solution.py:107
  297.4 314.5 %reduce-scatter.3.cloned.1.call-start = ((), (), s32[]{:S(2)}) async-start(), calls=%async_computation.2 | async-start | bytes 15728640 | tf_op jit(solution)/shard_map/reduce_scatter | solution.py:86
  327.5 18.3 %copy-start.1 = (f32[1024,1024]{1,0:T(8,128)S(1)}, f32[1024,1024]{1,0:T(8,128)}, u32[]{:S(2)}) copy-start(f32[1024,1024]{1,0:T(8,128)} %fusion.20) | copy-start | bytes 12582916
  368.5 19.1 %copy-start.7 = (f32[8,128,128]{2,1,0:T(8,128)S(1)}, f32[8,128,128]{2,1,0:T(8,128)}, u32[]{:S(2)}) copy-start(f32[8,128,128]{2,1,0:T(8,128)} %custom-call.1) | copy-start | bytes 1572868
  368.5 19.1 %copy-start.11 = (bf16[8]{0:T(256)(128)(2,1)S(1)}, bf16[8]{0:T(256)(128)(2,1)}, u32[]{:S(2)}) copy-start(bf16[8]{0:T(256)(128)(2,1)} %get-tuple-element.375) | copy-start | bytes 52
  387.6 31.1 %copy-start.10 = (s32[1024]{0:T(1024)S(1)}, s32[1024]{0:T(1024)}, u32[]{:S(2)}) copy-start(s32[1024]{0:T(1024)} %param.13) | copy-start | bytes 12292
  428.3 2.2 copy-start.2
  428.3 2.9 copy-start.5
Sparse Core Ops, SparseCore 0:
  23.8 28.0 all-gather.6
  276.2 25.5 all-gather.8
  305.3 91.9 reduce-scatter.4
  400.1 211.8 reduce-scatter.2
